TPU v7x, 32 devices: a whole 2x2x4 slice. The times are simulated.
32 devices in a mesh: cls: 4 (over y, x), str: 8 (over z, core).
Axes of the slice: x: 2, y: 2, z: 4, core: 2. Of those that a mesh axis runs over, the one named last changes fastest.
Arguments:
- first_factor_tiles: float32 [8, 1024, 2, 4, 1024], P(None, ('cls', 'str')), may hold values from -6 to 6
- b_blocks: float32 [8, 1024, 2, 4, 512], P(None, ('cls', 'str')), may hold values from -0.0625 to 0.0625
Outputs:
- c_blocks: float32 [8, 1024, 2, 4, 512], P(None, ('cls', 'str'))
All inputs are finite; a program needn't handle non-finite values.
Results may differ from a plain program's by a relative error of at most 0.0003.
Values sent between devices are 32-bit elements; how exact they have to be, the bound alone decides.
A program may use at most 128 MiB of HBM per device.

v0:
```python
import functools

import jax
import jax.numpy as jnp
from jax import lax
from jax.experimental import pallas as pl
from jax.experimental.pallas import tpu as pltpu
from jax.sharding import PartitionSpec as P

MESH = pl.DeviceIdType.MESH
LAG = 3
AHEAD = 2


def flip(index, mask, count):
    out, bit = index, 1
    while bit < count:
        have, want = (index // bit) % 2, (mask // bit) % 2
        out = out + want * (1 - 2 * have) * bit
        bit *= 2
    return out


def kernel(
    classes, subs, a_ref, b_ref, o_ref, aland, ball,
    ahi, alo, astage, bstage, bhi, blo, cpart, rland,
    a_send, a_recv, own_send, fwd_send, line_recv, peer_send, peer_recv,
    c_send, c_recv, a_load, b_load, o_sem,
):
    chunks, groups, piece, width = b_ref.shape
    rows = a_ref.shape[1]
    depth = subs * piece
    spots = subs // 2
    c, s = lax.axis_index("cls"), lax.axis_index("str")
    spot, core = s // 2, s % 2
    mate = (c, s + 1 - 2 * core)
    beside = ((c, s - 2), (c, s + 2))
    has = (spot > 0, spot < spots - 1)

    barrier = pltpu.get_barrier_semaphore()
    for d in range(1, classes):
        pl.semaphore_signal(barrier, inc=1, device_id=(flip(c, d, classes), s), device_id_type=MESH)
    pl.semaphore_signal(barrier, inc=1, device_id=mate, device_id_type=MESH)
    for side in range(2):
        @pl.when(has[side])
        def _():
            pl.semaphore_signal(barrier, inc=1, device_id=beside[side], device_id_type=MESH)
    lower, higher = (spot + spots - 1) // spots, (2 * spots - 2 - spot) // spots
    pl.semaphore_wait(barrier, classes + lower + higher)

    def remote(src, dst, send, recv, to):
        return pltpu.make_async_remote_copy(
            src_ref=src, dst_ref=dst, send_sem=send, recv_sem=recv,
            device_id=to, device_id_type=MESH,
        )

    def slot(j, owner):
        return ball.at[j, :, pl.ds(pl.multiple_of(owner * piece, piece), piece), :]

    def own_line(j, side):
        return remote(b_ref.at[j], slot(j, s), own_send.at[side, j], line_recv.at[side, j, 0], beside[side])

    def own_mate(j):
        return remote(b_ref.at[j], slot(j, s), peer_send.at[j, spot], peer_recv.at[j, spot], mate)

    def origin(side, dist):
        return spot + dist if side == 0 else spot - dist

    def there(side, dist):
        return spot + dist < spots if side == 0 else spot >= dist

    def arrival(j, side, dist):
        at = slot(j, 2 * origin(side, dist) + core)
        return remote(at, at, own_send.at[side, j], line_recv.at[side, j, dist - 1], beside[1 - side])

    def onward(j, side, dist):
        at = slot(j, 2 * origin(side, dist) + core)
        return remote(at, at, fwd_send.at[side, j, dist - 1], line_recv.at[side, j, dist], beside[side])

    def across(j, side, dist):
        begin = origin(side, dist)
        at = slot(j, 2 * begin + core)
        return remote(at, at, peer_send.at[j, begin], peer_recv.at[j, begin], mate)

    def forward(j, dist):
        for side in range(2):
            @pl.when(there(side, dist))
            def _():
                arrival(j, side, dist).wait_recv()

                @pl.when(has[side])
                def _():
                    onward(j, side, dist).start()

                across(j, side, dist).start()

    def a_copy(d):
        peer = flip(c, d, classes)
        return remote(
            a_ref.at[:, :, pl.ds(pl.multiple_of(peer * depth, depth), depth)],
            aland.at[:, pl.ds(pl.multiple_of(c * rows, rows), rows), :],
            a_send.at[d], a_recv.at[d], (peer, s),
        )

    for d in range(1, classes):
        a_copy(d).start()

    def begin(j, _):
        for side in range(2):
            @pl.when(has[side])
            def _():
                own_line(j, side).start()
        own_mate(j).start()
        return 0

    lax.fori_loop(0, chunks, begin, 0)

    for j in range(min(AHEAD, chunks)):
        forward(j, 1)
    for d in range(1, classes):
        a_copy(d).wait_recv()

    def load_a(g, held):
        for e in range(classes):
            to = astage.at[held, pl.ds(e * rows, rows), :]

            @pl.when(c == e)
            def _():
                pltpu.make_async_copy(
                    a_ref.at[g, :, pl.ds(pl.multiple_of(c * depth, depth), depth)], to, a_load.at[held]
                ).start()

            @pl.when(c != e)
            def _():
                pltpu.make_async_copy(aland.at[g, pl.ds(e * rows, rows), :], to, a_load.at[held]).start()

    load_a(0, 0)
    for g in range(groups):
        held = g % 2
        if g + 1 < groups:
            load_a(g + 1, 1 - held)
        pltpu.make_async_copy(aland.at[g], astage.at[held], a_load.at[held]).wait()

        def split(m, _, held=held, g=g):
            at = pl.ds(pl.multiple_of(m * rows, rows), rows)
            value = astage[held, at, :]
            high = value.astype(jnp.bfloat16)
            ahi[at, g * depth:(g + 1) * depth] = high
            alo[at, g * depth:(g + 1) * depth] = (value - high.astype(jnp.float32)).astype(jnp.bfloat16)
            return 0

        lax.fori_loop(0, classes, split, 0)

    def c_copy(j, d):
        peer = flip(c, d, classes)
        return remote(
            cpart.at[j, pl.ds(pl.multiple_of(peer * rows, rows), rows), :],
            rland.at[j, d - 1], c_send.at[j, d], c_recv.at[j, d], (peer, s),
        )

    mine = pl.ds(pl.multiple_of(c * rows, rows), rows)

    def out_copy(j):
        return pltpu.make_async_copy(cpart.at[j, mine, :], o_ref.at[j], o_sem.at[j])

    def reduce(j):
        for d in range(1, classes):
            c_copy(j, d).wait_recv()
        total = cpart[j, mine, :]
        for d in range(1, classes):
            total = total + rland[j, d - 1]
        cpart[j, mine, :] = total
        out_copy(j).start()

    def step(j, _):
        if spots > 1:
            @pl.when(j + AHEAD < chunks)
            def _():
                forward(j + AHEAD, 1)
        for dist in range(2, spots):
            forward(j, dist)

        for owner in range(subs):
            to = bstage.at[:, pl.ds(owner * piece, piece), :]

            @pl.when(s == owner)
            def _():
                pltpu.make_async_copy(b_ref.at[j], to, b_load.at[0]).start()

            @pl.when(s != owner)
            def _():
                @pl.when(core != owner % 2)
                def _():
                    remote(to_slot(j, owner), to_slot(j, owner), peer_send.at[j, owner // 2],
                           peer_recv.at[j, owner // 2], mate).wait_recv()

                pltpu.make_async_copy(to_slot(j, owner), to, b_load.at[0]).start()

        pltpu.make_async_copy(ball.at[j], bstage, b_load.at[0]).wait()

        def split(g, _):
            value = bstage[g]
            high = value.astype(jnp.bfloat16)
            at = pl.ds(pl.multiple_of(g * depth, depth), depth)
            bhi[at, :] = high
            blo[at, :] = (value - high.astype(jnp.float32)).astype(jnp.bfloat16)
            return 0

        lax.fori_loop(0, groups, split, 0)

        def part(i, _):
            d = (i + 1) % classes
            at = pl.ds(pl.multiple_of(flip(c, d, classes) * rows, rows), rows)
            dot = functools.partial(jnp.dot, preferred_element_type=jnp.float32)
            cpart[j, at, :] = (
                dot(ahi[at, :], bhi[...]) + dot(ahi[at, :], blo[...]) + dot(alo[at, :], bhi[...])
            )

            @pl.when(d != 0)
            def _():
                c_copy(j, d).start()

            return 0

        lax.fori_loop(0, classes, part, 0)

        @pl.when(j >= LAG)
        def _():
            reduce(j - LAG)

        return 0

    def to_slot(j, owner):
        return ball.at[j, :, pl.ds(owner * piece, piece), :]

    lax.fori_loop(0, chunks, step, 0)
    for j in range(max(chunks - LAG, 0), chunks):
        reduce(j)

    def finish(j, _):
        out_copy(j).wait()
        own_mate(j).wait_send()
        for d in range(1, classes):
            c_copy(j, d).wait_send()
        for side in range(2):
            @pl.when(has[side])
            def _():
                own_line(j, side).wait_send()
            for dist in range(1, spots):
                @pl.when(there(side, dist))
                def _():
                    @pl.when(has[side])
                    def _():
                        onward(j, side, dist).wait_send()
                    across(j, side, dist).wait_send()
        return 0

    lax.fori_loop(0, chunks, finish, 0)
    for d in range(1, classes):
        a_copy(d).wait_send()


def local(classes, subs, first_factor_tiles, b_blocks):
    blocks, q, halves, cols, order = first_factor_tiles.shape
    inner, width = halves * cols, b_blocks.shape[4]
    rows = blocks * q
    left = first_factor_tiles.reshape(rows, inner, order)
    right = jnp.transpose(b_blocks.reshape(inner, q, inner, width), (2, 0, 1, 3))
    if q % 8 == 0:
        left = jnp.transpose(left, (1, 0, 2))
    else:
        left = left.reshape(rows, inner, classes * subs, q)
        left = jnp.transpose(left, (0, 2, 1, 3)).reshape(1, rows, inner * order)
        right = right.reshape(inner, 1, inner * q, width)
    chunks, groups, piece, _ = right.shape
    depth = subs * piece
    dma = pltpu.SemaphoreType.DMA
    f32, bf16 = jnp.float32, jnp.bfloat16
    spots = subs // 2
    out, _, _ = pl.pallas_call(
        functools.partial(kernel, classes, subs),
        out_shape=(
            jax.ShapeDtypeStruct((chunks, rows, width), f32),
            jax.ShapeDtypeStruct((groups, classes * rows, depth), f32),
            jax.ShapeDtypeStruct((chunks, groups, depth, width), f32),
        ),
        in_specs=[pl.BlockSpec(memory_space=pl.ANY)] * 2,
        out_specs=(pl.BlockSpec(memory_space=pl.ANY),) * 3,
        scratch_shapes=[
            pltpu.VMEM((classes * rows, groups * depth), bf16),
            pltpu.VMEM((classes * rows, groups * depth), bf16),
            pltpu.VMEM((2, classes * rows, depth), f32),
            pltpu.VMEM((groups, depth, width), f32),
            pltpu.VMEM((groups * depth, width), bf16),
            pltpu.VMEM((groups * depth, width), bf16),
            pltpu.VMEM((chunks, classes * rows, width), f32),
            pltpu.VMEM((chunks, classes - 1, rows, width), f32),
            dma((classes,)),
            dma((classes,)),
            dma((2, chunks)),
            dma((2, chunks, spots)),
            dma((2, chunks, spots)),
            dma((chunks, spots)),
            dma((chunks, spots)),
            dma((chunks, classes)),
            dma((chunks, classes)),
            dma((2,)),
            dma((1,)),
            dma((chunks,)),
        ],
        compiler_params=pltpu.CompilerParams(
            collective_id=0, has_side_effects=True, vmem_limit_bytes=60 * 1024 * 1024
        ),
    )(left, right)
    out = jnp.transpose(out, (1, 0, 2))
    return out.reshape(b_blocks.shape)


def solution(mesh):
    spec = P(None, ("cls", "str"), None, None, None)
    return jax.shard_map(
        functools.partial(local, mesh.shape["cls"], mesh.shape["str"]),
        mesh=mesh, in_specs=(spec, spec), out_specs=spec, check_vma=False,
    )
```

profile of v0, /device:TPU:0, one launch (start us, length us, event | category | flops | bytes accessed | tf_op | source)
XLA Modules:
  0.0 355.0 jit_solution(9866168665643146471)
XLA Ops:
  0.0 0.0 copy-start
  0.0 6.8 %copy.4 = f32[8,32,2,4,512]{4,1,0,3,2:T(8,128)} copy(f32[8,32,2,4,512]{4,3,2,1,0:T(4,128)} %param.3) | data formatting | bytes 8388608 | tf_op args[1]
  6.8 0.0 copy-done
  6.8 8.1 %copy.3 = f32[8,32,2,4,1024]{4,1,0,3,2:T(8,128)} copy(f32[8,32,2,4,1024]{4,3,2,1,0:T(4,128)S(1)} %copy-done) | data formatting | bytes 16777216 | tf_op args[0]
  14.8 333.2 %shard_map.28 = (f32[8,256,512]{2,1,0:T(8,128)}, f32[8,1024,256]{2,1,0:T(8,128)}, f32[8,8,256,512]{3,2,1,0:T(8,128)}) custom-call(f32[8,256,1024]{2,1,0:T(8,128)} %bitcast.9, f32[8,8,32,512]{3,2,1,0:T(8,128)} %bitcast.10), custom_call_target="tpu_custom_call" | custom-call | tf_op jit(solution)/shard_map/pallas_call | solution.py:280
  348.1 6.9 %copy.5 = f32[8,32,2,4,512]{4,3,2,1,0:T(4,128)} copy(f32[8,32,2,4,512]{4,1,0,3,2:T(8,128)} %bitcast.11) | data formatting | bytes 8388608 | tf_op jit(solution)/shard_map/reshape | solution.py:316
Async XLA Ops:
  0.0 6.8 %copy-start = (f32[8,32,2,4,1024]{4,3,2,1,0:T(4,128)S(1)}, f32[8,32,2,4,1024]{4,3,2,1,0:T(4,128)}, u32[]{:S(2)}) copy-start(f32[8,32,2,4,1024]{4,3,2,1,0:T(4,128)} %param.2) | copy-start | bytes 25165828
where the time goes:
time: 356 us; the launch traced here: 355 us
  Pallas kernels  333 us (94%)
  local copies, waits for them, and re-layouts  21.8 us (6%)
    pallas_call x1, Pallas kernels, local(): pl.pallas_call(functools.partial(kernel, classes, subs), out_shape=(jax.S...  333 us
    unnamed x4, local copies, waits for them, and re-layouts  14.8 us

commit v1 on v0

--- a/solution.py
+++ b/solution.py
@@ -9,7 +9,11 @@
 
 MESH = pl.DeviceIdType.MESH
 LAG = 3
-AHEAD = 2
+EARLY = 2
+AHEAD = 6
+LEAD = 2
+LANE = 128
+SUBLANE = 8
 
 
 def flip(index, mask, count):
@@ -115,7 +119,7 @@
 
     lax.fori_loop(0, chunks, begin, 0)
 
-    for j in range(min(AHEAD, chunks)):
+    for j in range(min(EARLY, chunks)):
         forward(j, 1)
     for d in range(1, classes):
         a_copy(d).wait_recv()
@@ -174,9 +178,9 @@
 
     def step(j, _):
         if spots > 1:
-            @pl.when(j + AHEAD < chunks)
-            def _():
-                forward(j + AHEAD, 1)
+            @pl.when(j + EARLY < chunks)
+            def _():
+                forward(j + EARLY, 1)
         for dist in range(2, spots):
             forward(j, dist)
 
@@ -316,9 +320,415 @@
     return out.reshape(b_blocks.shape)
 
 
+def stream(
+    classes, subs, a_ref, b_ref, o_ref, aland, ball,
+    flat, bown, astage, ahi, alo, bstage, bhi, blo, cpart, rland,
+    a_send, a_recv, own_send, fwd_send, line_recv, peer_send, peer_recv, keep_sem,
+    c_send, c_recv, a_load, b_load, o_sem,
+):
+    lead, _, unit, lane = a_ref.shape
+    rows, ncol, _ = b_ref.shape
+    chunks, blocks, depth, width = ball.shape
+    bands = depth // lane
+    piece = depth // subs
+    per = width // lane
+    levels = classes.bit_length() - 1
+    spots = subs // 2
+    c, s = lax.axis_index("cls"), lax.axis_index("str")
+    spot, core = s // 2, s % 2
+    mate = (c, s + 1 - 2 * core)
+    beside = ((c, s - 2), (c, s + 2))
+    has = (spot > 0, spot < spots - 1)
+    inner = (spot > 0) & (spot < spots - 1)
+    outer = (spot == 0) | (spot == spots - 1)
+    near = spot // (spots // bands)
+
+    barrier = pltpu.get_barrier_semaphore()
+    for d in range(1, classes):
+        pl.semaphore_signal(barrier, inc=1, device_id=(flip(c, d, classes), s), device_id_type=MESH)
+    pl.semaphore_signal(barrier, inc=1, device_id=mate, device_id_type=MESH)
+    for side in range(2):
+        @pl.when(has[side])
+        def _():
+            pl.semaphore_signal(barrier, inc=1, device_id=beside[side], device_id_type=MESH)
+    b_in = pltpu.make_async_copy(b_ref, flat, b_load.at[0])
+    b_in.start()
+    lower, higher = (spot + spots - 1) // spots, (2 * spots - 2 - spot) // spots
+    pl.semaphore_wait(barrier, classes + lower + higher)
+
+    def remote(src, dst, send, recv, to):
+        return pltpu.make_async_remote_copy(
+            src_ref=src, dst_ref=dst, send_sem=send, recv_sem=recv,
+            device_id=to, device_id_type=MESH,
+        )
+
+    def a_copy(d):
+        peer = flip(c, d, classes)
+        return remote(a_ref.at[:, peer], aland.at[d - 1], a_send.at[d], a_recv.at[d], (peer, s))
+
+    for d in range(1, classes):
+        a_copy(d).start()
+
+    def slot(j, owner):
+        return ball.at[j, :, pl.ds(pl.multiple_of(owner * piece, piece), piece), :]
+
+    def own_line(j, side):
+        return remote(bown.at[j], slot(j, s), own_send.at[side, j], line_recv.at[side, j, 0], beside[side])
+
+    def own_mate(j):
+        return remote(bown.at[j], slot(j, s), peer_send.at[j, spot], peer_recv.at[j, spot], mate)
+
+    def own_keep(j):
+        return pltpu.make_async_copy(bown.at[j], slot(j, s), keep_sem.at[j])
+
+    def origin(side, dist):
+        return spot + dist if side == 0 else spot - dist
+
+    def there(side, dist):
+        return spot + dist < spots if side == 0 else spot >= dist
+
+    def arrival(j, side, dist):
+        at = slot(j, 2 * origin(side, dist) + core)
+        return remote(at, at, own_send.at[side, j], line_recv.at[side, j, dist - 1], beside[1 - side])
+
+    def onward(j, side, dist):
+        at = slot(j, 2 * origin(side, dist) + core)
+        return remote(at, at, fwd_send.at[side, j, dist - 1], line_recv.at[side, j, dist], beside[side])
+
+    def across(j, side, dist):
+        begin = origin(side, dist)
+        at = slot(j, 2 * begin + core)
+        return remote(at, at, peer_send.at[j, begin], peer_recv.at[j, begin], mate)
+
+    def forward(j, dist):
+        for side in range(2):
+            @pl.when(there(side, dist))
+            def _():
+                arrival(j, side, dist).wait_recv()
+
+                @pl.when(has[side])
+                def _():
+                    onward(j, side, dist).start()
+
+                across(j, side, dist).start()
+
+    def own_out(j):
+        for side in range(2):
+            @pl.when(has[side])
+            def _():
+                own_line(j, side).start()
+
+    b_in.wait()
+    rows_of = flat.reshape(rows * ncol, lane)
+
+    def lay(j):
+        for p in range(per):
+            value = rows_of[pl.ds(j * per + p, rows, stride=ncol), :]
+            bown[j, :, :, p * lane:(p + 1) * lane] = value.reshape(blocks, piece, lane)
+
+    for j in range(min(LEAD, chunks)):
+        lay(j)
+    for j in range(min(LEAD, chunks)):
+        own_out(j)
+
+    def lay_more(j, _):
+        lay(j)
+        return 0
+
+    lax.fori_loop(min(LEAD, chunks), chunks, lay_more, 0)
+
+    def begin(j, _):
+        own_mate(j).start()
+        own_keep(j).start()
+
+        @pl.when(outer & (j >= LEAD))
+        def _():
+            own_out(j)
+
+        return 0
+
+    lax.fori_loop(0, chunks, begin, 0)
+
+    def take_a(d):
+        held = astage.at[d % 2]
+        if d == 0:
+            return pltpu.make_async_copy(a_ref.at[:, c], held, a_load.at[0])
+        return pltpu.make_async_copy(aland.at[d - 1], held, a_load.at[d % 2])
+
+    def split_a(d):
+        lines = astage.at[d % 2].reshape(lead * unit, lane)
+        stride = lead * unit // rows
+        cols = unit // bands
+
+        def one(k, _):
+            h, band, col = k // unit, (k % unit) // cols, k % cols
+            value = lines[pl.ds(k, rows, stride=stride), :]
+            high = value.astype(jnp.bfloat16)
+            at = pl.ds(pl.multiple_of((h * cols + col) * lane, lane), lane)
+            ahi[band, d * rows:(d + 1) * rows, at] = high
+            alo[band, d * rows:(d + 1) * rows, at] = (value - high.astype(jnp.float32)).astype(jnp.bfloat16)
+            return 0
+
+        lax.fori_loop(0, stride, one, 0)
+
+    take_a(0).start()
+    take_a(0).wait()
+    split_a(0)
+
+    @pl.when(inner)
+    def _():
+        def early(j, _):
+            for dist in range(1, spots):
+                forward(j, dist)
+
+            @pl.when(j + LEAD < chunks)
+            def _():
+                own_out(j + LEAD)
+
+            return 0
+
+        lax.fori_loop(0, min(AHEAD, chunks), early, 0)
+
+    for d in range(1, classes):
+        a_copy(d).wait_recv()
+        take_a(d).start()
+        if d > 1:
+            take_a(d - 1).wait()
+            split_a(d - 1)
+    take_a(classes - 1).wait()
+    split_a(classes - 1)
+
+    def order(p):
+        return [(p + i) % levels for i in range(levels)]
+
+    def place(p, d):
+        at = 0
+        for bit in order(p):
+            at = 2 * at + (d // (1 << bit)) % 2
+        return at
+
+    def c_copy(j, p, level):
+        count = classes >> (level + 1)
+        peer = flip(c, 1 << order(p)[level], classes)
+        return remote(
+            cpart.at[j, p, pl.ds(count, count)],
+            rland.at[j, p, pl.ds(classes - 2 * count, count)],
+            c_send.at[j, p, level], c_recv.at[j, p, level], (peer, s),
+        )
+
+    share = ncol // o_sem.shape[0]
+
+    def out_copy(g):
+        at = pl.ds(pl.multiple_of(g * share, share), share)
+        return pltpu.make_async_copy(flat.at[:, at, :], o_ref.at[:, at, :], o_sem.at[g])
+
+    def reduce(j, level):
+        count = classes >> (level + 1)
+        for p in range(per):
+            c_copy(j, p, level).wait_recv()
+            if level + 1 < levels:
+                cpart[j, p, 0:count] = (
+                    cpart[j, p, 0:count] + rland[j, p, classes - 2 * count:classes - count]
+                )
+                c_copy(j, p, level + 1).start()
+            else:
+                rows_of[pl.ds(j * per + p, rows, stride=ncol), :] = (
+                    cpart[j, p, 0] + rland[j, p, classes - 2]
+                )
+        if level + 1 == levels:
+            @pl.when((j + 1) % (share // per) == 0)
+            def _():
+                out_copy((j + 1) // (share // per) - 1).start()
+
+    def hold(j, band):
+        for owner in range(subs):
+            @pl.when(owner // (subs // bands) == band)
+            def _():
+                @pl.when(s == owner)
+                def _():
+                    own_keep(j).wait()
+
+                @pl.when(core != owner % 2)
+                def _():
+                    at = slot(j, owner)
+                    remote(at, at, peer_send.at[j, owner // 2], peer_recv.at[j, owner // 2], mate).wait_recv()
+
+        take = pltpu.make_async_copy(
+            ball.at[j, :, pl.ds(pl.multiple_of(band * lane, lane), lane), :], bstage, b_load.at[0]
+        )
+        take.start()
+        take.wait()
+
+        def split(g, _):
+            value = bstage[g]
+            high = value.astype(jnp.bfloat16)
+            at = pl.ds(pl.multiple_of(g * lane, lane), lane)
+            bhi[at, :] = high
+            blo[at, :] = (value - high.astype(jnp.float32)).astype(jnp.bfloat16)
+            return 0
+
+        lax.fori_loop(0, blocks, split, 0)
+
+    def multiply(j, band, first):
+        dot = functools.partial(jnp.dot, preferred_element_type=jnp.float32)
+
+        def part(d, _):
+            at = pl.ds(pl.multiple_of(d * rows, rows), rows)
+            high, low = ahi[band, at, :], alo[band, at, :]
+            total = dot(high, bhi[...]) + dot(high, blo[...]) + dot(low, bhi[...])
+            for p in range(per):
+                value = total[:, p * lane:(p + 1) * lane]
+                to = place(p, d)
+                cpart[j, p, to] = value if first else cpart[j, p, to] + value
+            return 0
+
+        lax.fori_loop(0, classes, part, 0)
+
+    def step(j, _):
+        @pl.when(inner & (j + AHEAD < chunks))
+        def _():
+            for dist in range(1, spots):
+                forward(j + AHEAD, dist)
+
+            @pl.when(j + AHEAD + LEAD < chunks)
+            def _():
+                own_out(j + AHEAD + LEAD)
+
+        @pl.when(outer)
+        def _():
+            forward(j, 1)
+
+        hold(j, near)
+        multiply(j, near, True)
+
+        @pl.when(j >= 1)
+        def _():
+            reduce(j - 1, 0)
+
+        if levels > 1:
+            @pl.when(j >= 2)
+            def _():
+                for level in range(1, levels):
+                    reduce(j - 2, level)
+
+        @pl.when(outer)
+        def _():
+            for dist in range(2, spots):
+                forward(j, dist)
+
+        for k in range(1, bands):
+            band = (near + k) % bands
+            hold(j, band)
+            multiply(j, band, False)
+        for p in range(per):
+            c_copy(j, p, 0).start()
+        return 0
+
+    lax.fori_loop(0, chunks, step, 0)
+    for level in range(1, levels):
+        reduce(chunks - 2, level)
+    for level in range(levels):
+        reduce(chunks - 1, level)
+    for g in range(o_sem.shape[0]):
+        out_copy(g).wait()
+
+    def finish(j, _):
+        own_mate(j).wait_send()
+        for p in range(per):
+            for level in range(levels):
+                c_copy(j, p, level).wait_send()
+        for side in range(2):
+            @pl.when(has[side])
+            def _():
+                own_line(j, side).wait_send()
+            for dist in range(1, spots):
+                @pl.when(there(side, dist))
+                def _():
+                    @pl.when(has[side])
+                    def _():
+                        onward(j, side, dist).wait_send()
+                    across(j, side, dist).wait_send()
+        return 0
+
+    lax.fori_loop(0, chunks, finish, 0)
+    for d in range(1, classes):
+        a_copy(d).wait_send()
+
+
+def streamed(classes, subs, first_factor_tiles, b_blocks):
+    blocks, q, halves, cols, order = first_factor_tiles.shape
+    wide = b_blocks.shape[4]
+    lane, sub = LANE, SUBLANE
+    rows, bands, ncol = blocks * q, order // (LANE * classes), halves * cols * wide // LANE
+    left = first_factor_tiles.reshape(rows, halves, cols, classes * bands, lane)
+    left = jnp.transpose(left, (0, 1, 3, 2, 4)).reshape(rows * halves, classes, bands * cols, lane)
+    right = b_blocks.reshape(rows, halves, cols, wide // lane, lane)
+    right = jnp.transpose(right, (0, 1, 3, 2, 4)).reshape(rows, ncol, lane)
+    lead, unit = rows * halves, bands * cols
+    per = 2
+    chunks, width, depth = ncol // per, per * lane, bands * lane
+    dma = pltpu.SemaphoreType.DMA
+    f32, bf16 = jnp.float32, jnp.bfloat16
+    spots, levels = subs // 2, classes.bit_length() - 1
+    out, _, _ = pl.pallas_call(
+        functools.partial(stream, classes, subs),
+        out_shape=(
+            jax.ShapeDtypeStruct((rows, ncol, lane), f32),
+            jax.ShapeDtypeStruct((classes - 1, lead, unit, lane), f32),
+            jax.ShapeDtypeStruct((chunks, blocks, depth, width), f32),
+        ),
+        in_specs=[pl.BlockSpec(memory_space=pl.ANY)] * 2,
+        out_specs=(pl.BlockSpec(memory_space=pl.ANY),) * 3,
+        scratch_shapes=[
+            pltpu.VMEM((rows, ncol, lane), f32),
+            pltpu.VMEM((chunks, blocks, q, width), f32),
+            pltpu.VMEM((2, lead, unit, lane), f32),
+            pltpu.VMEM((bands, classes * rows, blocks * lane), bf16),
+            pltpu.VMEM((bands, classes * rows, blocks * lane), bf16),
+            pltpu.VMEM((blocks, lane, width), f32),
+            pltpu.VMEM((blocks * lane, width), bf16),
+            pltpu.VMEM((blocks * lane, width), bf16),
+            pltpu.VMEM((chunks, per, classes, rows, lane), f32),
+            pltpu.VMEM((chunks, per, classes - 1, rows, lane), f32),
+            dma((classes,)),
+            dma((classes,)),
+            dma((2, chunks)),
+            dma((2, chunks, spots)),
+            dma((2, chunks, spots)),
+            dma((chunks, spots)),
+            dma((chunks, spots)),
+            dma((chunks,)),
+            dma((chunks, per, levels)),
+            dma((chunks, per, levels)),
+            dma((2,)),
+            dma((1,)),
+            dma((ncol // sub,)),
+        ],
+        compiler_params=pltpu.CompilerParams(
+            collective_id=0, has_side_effects=True, vmem_limit_bytes=60 * 1024 * 1024
+        ),
+    )(left, right)
+    out = out.reshape(rows, halves, wide // lane, cols, lane)
+    return jnp.transpose(out, (0, 1, 3, 2, 4)).reshape(b_blocks.shape)
+
+
+def fits(classes, subs, first_factor_tiles, b_blocks):
+    blocks, q, halves, cols, order = first_factor_tiles.shape
+    bands, spots = order // (LANE * classes), subs // 2
+    return (
+        q % SUBLANE == 0 and order % (LANE * classes) == 0 and (bands * cols) % SUBLANE == 0
+        and bands * LANE == subs * q and spots % bands == 0
+    )
+
+
+def either(classes, subs, first_factor_tiles, b_blocks):
+    pick = streamed if fits(classes, subs, first_factor_tiles, b_blocks) else local
+    return pick(classes, subs, first_factor_tiles, b_blocks)
+
+
 def solution(mesh):
     spec = P(None, ("cls", "str"), None, None, None)
     return jax.shard_map(
-        functools.partial(local, mesh.shape["cls"], mesh.shape["str"]),
+        functools.partial(either, mesh.shape["cls"], mesh.shape["str"]),
         mesh=mesh, in_specs=(spec, spec), out_specs=spec, check_vma=False,
     )

time: 356 us -> 339 us (0.952)
  local copies, waits for them, and re-layouts: 21.8 us -> 5.24 us
    unnamed x4 -> x1, local copies, waits for them, and re-layouts: 14.8 us -> 5.24 us
    reshape x1 -> x0, local copies, waits for them, and re-layouts: 6.93 us -> none  [local(): return out.reshape(b_blocks.shape)]
where the time goes in v1:
time: 339 us; the launch traced here: 338 us
  Pallas kernels  332 us (98%)
  local copies, waits for them, and re-layouts  5.24 us (2%)
    pallas_call x1, Pallas kernels, streamed(): pl.pallas_call(functools.partial(stream, classes, subs), out_shape=(jax.S...  332 us

profile of v1, /device:TPU:0, one launch (start us, length us, event | category | flops | bytes accessed | tf_op | source)
XLA Modules:
  0.0 337.5 jit_solution(2985843269133736214)
XLA Ops:
  0.0 332.3 %shard_map.28 = (f32[256,32,128]{2,1,0:T(8,128)}, f32[3,512,8,128]{3,2,1,0:T(8,128)}, f32[16,8,256,256]{3,2,1,0:T(8,128)}) custom-call(f32[512,4,8,128]{3,2,1,0:T(8,128)} %bitcast.15, f32[256,32,128]{2,1,0:T(8,128)} %bitcast.16), custom_call_target="tpu_custom_call" | custom-call | tf_op jit(solution)/shard_map/pallas_call | solution.py:673
  332.3 5.2 %copy.7 = f32[8,32,2,4,512]{4,3,2,1,0:T(4,128)} copy(f32[8,32,2,4,512]{4,3,2,1,0:T(4,128)} %bitcast.17) | data formatting | bytes 8388608

commit v2 on v1

--- a/solution.py
+++ b/solution.py
@@ -12,6 +12,7 @@
 EARLY = 2
 AHEAD = 6
 LEAD = 2
+CALM = 10
 LANE = 128
 SUBLANE = 8
 
@@ -540,7 +541,7 @@
             def _():
                 out_copy((j + 1) // (share // per) - 1).start()
 
-    def hold(j, band):
+    def gather(j, band):
         for owner in range(subs):
             @pl.when(owner // (subs // bands) == band)
             def _():
@@ -553,14 +554,13 @@
                     at = slot(j, owner)
                     remote(at, at, peer_send.at[j, owner // 2], peer_recv.at[j, owner // 2], mate).wait_recv()
 
-        take = pltpu.make_async_copy(
-            ball.at[j, :, pl.ds(pl.multiple_of(band * lane, lane), lane), :], bstage, b_load.at[0]
-        )
-        take.start()
-        take.wait()
-
+    def take_b(j, band, held):
+        at = pl.ds(pl.multiple_of(band * lane, lane), lane)
+        return pltpu.make_async_copy(ball.at[j, :, at, :], bstage.at[held], b_load.at[held])
+
+    def split_b(held):
         def split(g, _):
-            value = bstage[g]
+            value = bstage[held, g]
             high = value.astype(jnp.bfloat16)
             at = pl.ds(pl.multiple_of(g * lane, lane), lane)
             bhi[at, :] = high
@@ -584,6 +584,23 @@
 
         lax.fori_loop(0, classes, part, 0)
 
+    def sum_first(k, _):
+        reduce(k, 0)
+        return 0
+
+    def sum_rest(k, _):
+        for level in range(1, levels):
+            reduce(k, level)
+        return 0
+
+    calm = jnp.where(outer, chunks * CALM // 16, chunks)
+
+    def first_sums(j):
+        return jnp.where(j > calm, j, jnp.maximum(j - 1, 0))
+
+    def last_sums(j):
+        return jnp.where(j > calm, j, jnp.maximum(j - 2, 0))
+
     def step(j, _):
         @pl.when(inner & (j + AHEAD < chunks))
         def _():
@@ -598,18 +615,12 @@
         def _():
             forward(j, 1)
 
-        hold(j, near)
+        gather(j, near)
+        take_b(j, near, 0).start()
+        lax.fori_loop(first_sums(j - 1), first_sums(j), sum_first, 0)
+        take_b(j, near, 0).wait()
+        split_b(0)
         multiply(j, near, True)
-
-        @pl.when(j >= 1)
-        def _():
-            reduce(j - 1, 0)
-
-        if levels > 1:
-            @pl.when(j >= 2)
-            def _():
-                for level in range(1, levels):
-                    reduce(j - 2, level)
 
         @pl.when(outer)
         def _():
@@ -618,17 +629,20 @@
 
         for k in range(1, bands):
             band = (near + k) % bands
-            hold(j, band)
+            gather(j, band)
+            take_b(j, band, k % 2).start()
+            if k == 1:
+                lax.fori_loop(last_sums(j - 1), last_sums(j), sum_rest, 0)
+            take_b(j, band, k % 2).wait()
+            split_b(k % 2)
             multiply(j, band, False)
         for p in range(per):
             c_copy(j, p, 0).start()
         return 0
 
     lax.fori_loop(0, chunks, step, 0)
-    for level in range(1, levels):
-        reduce(chunks - 2, level)
-    for level in range(levels):
-        reduce(chunks - 1, level)
+    lax.fori_loop(first_sums(chunks - 1), chunks, sum_first, 0)
+    lax.fori_loop(last_sums(chunks - 1), chunks, sum_rest, 0)
     for g in range(o_sem.shape[0]):
         out_copy(g).wait()
 
@@ -685,7 +699,7 @@
             pltpu.VMEM((2, lead, unit, lane), f32),
             pltpu.VMEM((bands, classes * rows, blocks * lane), bf16),
             pltpu.VMEM((bands, classes * rows, blocks * lane), bf16),
-            pltpu.VMEM((blocks, lane, width), f32),
+            pltpu.VMEM((2, blocks, lane, width), f32),
             pltpu.VMEM((blocks * lane, width), bf16),
             pltpu.VMEM((blocks * lane, width), bf16),
             pltpu.VMEM((chunks, per, classes, rows, lane), f32),
@@ -701,7 +715,7 @@
             dma((chunks, per, levels)),
             dma((chunks, per, levels)),
             dma((2,)),
-            dma((1,)),
+            dma((2,)),
             dma((ncol // sub,)),
         ],
         compiler_params=pltpu.CompilerParams(
@@ -716,7 +730,7 @@
     blocks, q, halves, cols, order = first_factor_tiles.shape
     bands, spots = order // (LANE * classes), subs // 2
     return (
-        q % SUBLANE == 0 and order % (LANE * classes) == 0 and (bands * cols) % SUBLANE == 0
+        classes > 1 and bands > 1 and q % SUBLANE == 0 and order % (LANE * classes) == 0 and (bands * cols) % SUBLANE == 0
         and bands * LANE == subs * q and spots % bands == 0
     )
 

time: 339 us -> 325 us (0.959)
  Pallas kernels: 332 us -> 318 us
    pallas_call x1, Pallas kernels: 332 us -> 318 us  [streamed(): pl.pallas_call(functools.partial(stream, classes, subs), out_shape=(jax.S...]
where the time goes in v2:
time: 325 us; the launch traced here: 323 us
  Pallas kernels  318 us (98%)
  local copies, waits for them, and re-layouts  5.24 us (2%)
    pallas_call x1, Pallas kernels, streamed(): pl.pallas_call(functools.partial(stream, classes, subs), out_shape=(jax.S...  318 us

profile of v2, /device:TPU:0, one launch (start us, length us, event | category | flops | bytes accessed | tf_op | source)
XLA Modules:
  0.0 323.2 jit_solution(5709355101485424984)
XLA Ops:
  0.0 318.0 %shard_map.28 = (f32[256,32,128]{2,1,0:T(8,128)}, f32[3,512,8,128]{3,2,1,0:T(8,128)}, f32[16,8,256,256]{3,2,1,0:T(8,128)}) custom-call(f32[512,4,8,128]{3,2,1,0:T(8,128)} %bitcast.15, f32[256,32,128]{2,1,0:T(8,128)} %bitcast.16), custom_call_target="tpu_custom_call" | custom-call | tf_op jit(solution)/shard_map/pallas_call | solution.py:687
  318.0 5.2 %copy.7 = f32[8,32,2,4,512]{4,3,2,1,0:T(4,128)} copy(f32[8,32,2,4,512]{4,3,2,1,0:T(4,128)} %bitcast.17) | data formatting | bytes 8388608

commit v3 on v2

--- a/solution.py
+++ b/solution.py
@@ -10,9 +10,12 @@
 MESH = pl.DeviceIdType.MESH
 LAG = 3
 EARLY = 2
-AHEAD = 6
+AHEAD = 7
 LEAD = 2
-CALM = 10
+MORE = 2
+GIVEN = 2
+SLOTS = 8
+CALM = 14
 LANE = 128
 SUBLANE = 8
 
@@ -322,9 +325,9 @@
 
 
 def stream(
-    classes, subs, a_ref, b_ref, o_ref, aland, ball,
-    flat, bown, astage, ahi, alo, bstage, bhi, blo, cpart, rland,
-    a_send, a_recv, own_send, fwd_send, line_recv, peer_send, peer_recv, keep_sem,
+    classes, subs, given, a_ref, b_ref, o_ref, aland, ball,
+    flat, bown, astage, ahi, alo, bstage, bhi, blo, cpart, rland, lent, hhi, hlo, back,
+    a_send, a_recv, lend_send, lend_recv, back_send, back_recv, own_send, fwd_send, line_recv, peer_send, peer_recv, keep_sem,
     c_send, c_recv, a_load, b_load, o_sem,
 ):
     lead, _, unit, lane = a_ref.shape
@@ -343,6 +346,11 @@
     inner = (spot > 0) & (spot < spots - 1)
     outer = (spot == 0) | (spot == spots - 1)
     near = spot // (spots // bands)
+    slots = cpart.shape[0]
+    helps = (spot == 1) | (spot == spots - 2)
+    total = jnp.where(helps, chunks + given, chunks)
+    ends = (spot == 1, spot == spots - 2)
+    friend = (c, jnp.where((spot == 0) | (spot == spots - 2), s + 2, s - 2))
 
     barrier = pltpu.get_barrier_semaphore()
     for d in range(1, classes):
@@ -403,21 +411,39 @@
 
     def forward(j, dist):
         for side in range(2):
-            @pl.when(there(side, dist))
+            @pl.when(gets(j, side, dist))
             def _():
                 arrival(j, side, dist).wait_recv()
 
-                @pl.when(has[side])
+                @pl.when(feeds(j, side))
                 def _():
                     onward(j, side, dist).start()
 
                 across(j, side, dist).start()
 
+    def relay(t):
+        for dist in range(1, spots):
+            @pl.when((t - dist + 1 >= 0) & (t - dist + 1 < chunks))
+            def _():
+                forward(t - dist + 1, dist)
+
+    def feeds(j, side):
+        return has[side] & ((j >= given) | jnp.logical_not(ends[side]))
+
+    def gets(j, side, dist):
+        return there(side, dist) & ((j >= given) | inner)
+
+    shift = given + MORE
+
     def own_out(j):
         for side in range(2):
-            @pl.when(has[side])
+            @pl.when(has[side] & jnp.logical_not(ends[side]))
             def _():
                 own_line(j, side).start()
+
+            @pl.when(ends[side] & (j + shift < chunks))
+            def _():
+                own_line(j + shift, side).start()
 
     b_in.wait()
     rows_of = flat.reshape(rows * ncol, lane)
@@ -427,8 +453,14 @@
             value = rows_of[pl.ds(j * per + p, rows, stride=ncol), :]
             bown[j, :, :, p * lane:(p + 1) * lane] = value.reshape(blocks, piece, lane)
 
-    for j in range(min(LEAD, chunks)):
+    first = min(LEAD + shift, chunks)
+    for j in range(first):
         lay(j)
+    for side in range(2):
+        for j in range(given, min(given + MORE, chunks)):
+            @pl.when(ends[side])
+            def _():
+                own_line(j, side).start()
     for j in range(min(LEAD, chunks)):
         own_out(j)
 
@@ -436,7 +468,7 @@
         lay(j)
         return 0
 
-    lax.fori_loop(min(LEAD, chunks), chunks, lay_more, 0)
+    lax.fori_loop(first, chunks, lay_more, 0)
 
     def begin(j, _):
         own_mate(j).start()
@@ -472,15 +504,53 @@
 
         lax.fori_loop(0, stride, one, 0)
 
+    def lend_copy(d):
+        return remote(lent.at[d], lent.at[d], lend_send.at[d], lend_recv.at[d], friend)
+
+    def lend(d):
+        if not given:
+            return
+        lines = astage.at[d % 2].reshape(lead * unit, lane)
+        stride = lead * unit // rows
+        cols = unit // bands
+        left = lax.broadcasted_iota(jnp.int32, (rows, lane), 1) < lane // 2
+        low = spot % 2 == 1
+
+        def block(g, band):
+            return lines[pl.ds((g // cols) * unit + band * cols + g % cols, rows, stride=stride), :]
+
+        @pl.when(outer)
+        def _():
+            for k in range(1, bands):
+                def whole(g, _, k=k):
+                    at = pl.ds(pl.multiple_of(((k - 1) * blocks + g) * lane, lane), lane)
+                    lent[d, :, at] = block(g, (near + k) % bands)
+                    return 0
+
+                lax.fori_loop(0, blocks, whole, 0)
+
+            def pair(g, _):
+                one, two = block(2 * g, near), block(2 * g + 1, near)
+                at = pl.ds(pl.multiple_of(((bands - 1) * blocks + g) * lane, lane), lane)
+                lent[d, :, at] = jnp.where(
+                    left,
+                    jnp.where(low, one, pltpu.roll(one, lane // 2, 1)),
+                    jnp.where(low, pltpu.roll(two, lane // 2, 1), two),
+                )
+                return 0
+
+            lax.fori_loop(0, blocks // 2, pair, 0)
+            lend_copy(d).start()
+
     take_a(0).start()
     take_a(0).wait()
     split_a(0)
+    lend(0)
 
     @pl.when(inner)
     def _():
         def early(j, _):
-            for dist in range(1, spots):
-                forward(j, dist)
+            relay(j)
 
             @pl.when(j + LEAD < chunks)
             def _():
@@ -496,8 +566,10 @@
         if d > 1:
             take_a(d - 1).wait()
             split_a(d - 1)
+            lend(d - 1)
     take_a(classes - 1).wait()
     split_a(classes - 1)
+    lend(classes - 1)
 
     def order(p):
         return [(p + i) % levels for i in range(levels)]
@@ -512,7 +584,7 @@
         count = classes >> (level + 1)
         peer = flip(c, 1 << order(p)[level], classes)
         return remote(
-            cpart.at[j, p, pl.ds(count, count)],
+            cpart.at[j % slots, p, pl.ds(count, count)],
             rland.at[j, p, pl.ds(classes - 2 * count, count)],
             c_send.at[j, p, level], c_recv.at[j, p, level], (peer, s),
         )
@@ -523,23 +595,44 @@
         at = pl.ds(pl.multiple_of(g * share, share), share)
         return pltpu.make_async_copy(flat.at[:, at, :], o_ref.at[:, at, :], o_sem.at[g])
 
+    late = -(-given * per // share)
+
+    def back_copy(i):
+        return remote(back.at[i], back.at[i], back_send.at[i], back_recv.at[i], friend)
+
     def reduce(j, level):
         count = classes >> (level + 1)
+        held = j % slots
         for p in range(per):
             c_copy(j, p, level).wait_recv()
             if level + 1 < levels:
-                cpart[j, p, 0:count] = (
-                    cpart[j, p, 0:count] + rland[j, p, classes - 2 * count:classes - count]
+                cpart[held, p, 0:count] = (
+                    cpart[held, p, 0:count] + rland[j, p, classes - 2 * count:classes - count]
                 )
                 c_copy(j, p, level + 1).start()
-            else:
+                continue
+
+            @pl.when(j < chunks)
+            def _():
                 rows_of[pl.ds(j * per + p, rows, stride=ncol), :] = (
-                    cpart[j, p, 0] + rland[j, p, classes - 2]
+                    cpart[held, p, 0] + rland[j, p, classes - 2]
                 )
+
+            if given:
+                @pl.when(j >= chunks)
+                def _():
+                    back[j - chunks, p] = cpart[held, p, 0] + rland[j, p, classes - 2]
         if level + 1 == levels:
-            @pl.when((j + 1) % (share // per) == 0)
-            def _():
-                out_copy((j + 1) // (share // per) - 1).start()
+            group = (j + 1) // (share // per) - 1
+
+            @pl.when((j < chunks) & ((j + 1) % (share // per) == 0) & (inner | (group >= late)))
+            def _():
+                out_copy(group).start()
+
+            if given:
+                @pl.when(j >= chunks)
+                def _():
+                    back_copy(j - chunks).start()
 
     def gather(j, band):
         for owner in range(subs):
@@ -549,7 +642,7 @@
                 def _():
                     own_keep(j).wait()
 
-                @pl.when(core != owner % 2)
+                @pl.when((core != owner % 2) & (inner | (j >= given) | (spot == owner // 2)))
                 def _():
                     at = slot(j, owner)
                     remote(at, at, peer_send.at[j, owner // 2], peer_recv.at[j, owner // 2], mate).wait_recv()
@@ -558,31 +651,60 @@
         at = pl.ds(pl.multiple_of(band * lane, lane), lane)
         return pltpu.make_async_copy(ball.at[j, :, at, :], bstage.at[held], b_load.at[held])
 
-    def split_b(held):
+    def split_b(held, size=lane, begin=0, step=lane):
         def split(g, _):
-            value = bstage[held, g]
+            value = bstage[held, g, 0:size, :]
             high = value.astype(jnp.bfloat16)
-            at = pl.ds(pl.multiple_of(g * lane, lane), lane)
+            at = pl.ds(pl.multiple_of(g * step + begin, size), size)
             bhi[at, :] = high
             blo[at, :] = (value - high.astype(jnp.float32)).astype(jnp.bfloat16)
             return 0
 
         lax.fori_loop(0, blocks, split, 0)
 
-    def multiply(j, band, first):
+    part_rows = 2 * piece
+
+    def take_part(j, held):
+        at = pl.ds(pl.multiple_of(spot * part_rows, part_rows), part_rows)
+        return pltpu.make_async_copy(
+            ball.at[j, :, at, :], bstage.at[held, :, pl.ds(0, part_rows), :], b_load.at[held]
+        )
+
+    def clear_part(begin):
+        def clear(g, _):
+            at = pl.ds(pl.multiple_of(g * lane + begin, part_rows), part_rows)
+            bhi[at, :] = jnp.zeros((part_rows, width), jnp.bfloat16)
+            blo[at, :] = jnp.zeros((part_rows, width), jnp.bfloat16)
+            return 0
+
+        lax.fori_loop(0, blocks, clear, 0)
+
+    def settle(j):
+        for p in range(per):
+            for level in range(levels):
+                c_copy(j, p, level).wait_send()
+
+    def multiply(j, left, deep, first):
         dot = functools.partial(jnp.dot, preferred_element_type=jnp.float32)
+        held = j % slots
 
         def part(d, _):
             at = pl.ds(pl.multiple_of(d * rows, rows), rows)
-            high, low = ahi[band, at, :], alo[band, at, :]
-            total = dot(high, bhi[...]) + dot(high, blo[...]) + dot(low, bhi[...])
+            high, low = left(at)
+            total = dot(high, bhi[0:deep]) + dot(high, blo[0:deep]) + dot(low, bhi[0:deep])
             for p in range(per):
                 value = total[:, p * lane:(p + 1) * lane]
                 to = place(p, d)
-                cpart[j, p, to] = value if first else cpart[j, p, to] + value
+                cpart[held, p, to] = value if first else cpart[held, p, to] + value
             return 0
 
         lax.fori_loop(0, classes, part, 0)
+
+    def mine(band):
+        return lambda at: (ahi[band, at, :], alo[band, at, :])
+
+    def theirs(begin, deep):
+        return lambda at: (hhi[at, begin:begin + deep], hlo[at, begin:begin + deep])
 
     def sum_first(k, _):
         reduce(k, 0)
@@ -593,7 +715,7 @@
             reduce(k, level)
         return 0
 
-    calm = jnp.where(outer, chunks * CALM // 16, chunks)
+    calm = jnp.where(outer, chunks * CALM // 16, chunks + given)
 
     def first_sums(j):
         return jnp.where(j > calm, j, jnp.maximum(j - 1, 0))
@@ -601,11 +723,13 @@
     def last_sums(j):
         return jnp.where(j > calm, j, jnp.maximum(j - 2, 0))
 
+    def sums(body, begin, end):
+        lax.fori_loop(begin, jnp.maximum(begin, end), body, 0)
+
     def step(j, _):
-        @pl.when(inner & (j + AHEAD < chunks))
-        def _():
-            for dist in range(1, spots):
-                forward(j + AHEAD, dist)
+        @pl.when(inner)
+        def _():
+            relay(j + AHEAD)
 
             @pl.when(j + AHEAD + LEAD < chunks)
             def _():
@@ -615,58 +739,163 @@
         def _():
             forward(j, 1)
 
+        alone = outer & (j < given)
+        whole = inner | (j >= given)
         gather(j, near)
-        take_b(j, near, 0).start()
-        lax.fori_loop(first_sums(j - 1), first_sums(j), sum_first, 0)
-        take_b(j, near, 0).wait()
-        split_b(0)
-        multiply(j, near, True)
+
+        @pl.when(whole)
+        def _():
+            take_b(j, near, 0).start()
+
+        if given:
+            @pl.when(alone)
+            def _():
+                take_part(j, 0).start()
+
+        sums(sum_first, first_sums(j - 1), j - 1)
+
+        @pl.when(j >= slots)
+        def _():
+            settle(j - slots)
+
+        @pl.when(whole)
+        def _():
+            take_b(j, near, 0).wait()
+            split_b(0)
+
+        if given:
+            @pl.when(alone)
+            def _():
+                take_part(j, 0).wait()
+                split_b(0, part_rows, (spot % 2) * part_rows)
+                clear_part((1 - spot % 2) * part_rows)
+
+        multiply(j, mine(near), blocks * lane, True)
+        sums(sum_first, jnp.maximum(j - 1, 0), first_sums(j))
 
         @pl.when(outer)
         def _():
             for dist in range(2, spots):
                 forward(j, dist)
 
-        for k in range(1, bands):
-            band = (near + k) % bands
-            gather(j, band)
-            take_b(j, band, k % 2).start()
-            if k == 1:
-                lax.fori_loop(last_sums(j - 1), last_sums(j), sum_rest, 0)
-            take_b(j, band, k % 2).wait()
-            split_b(k % 2)
-            multiply(j, band, False)
+        sums(sum_rest, last_sums(j - 1), j - 2)
+
+        @pl.when(whole)
+        def _():
+            for k in range(1, bands):
+                band = (near + k) % bands
+                gather(j, band)
+                take_b(j, band, k % 2).start()
+                take_b(j, band, k % 2).wait()
+                split_b(k % 2)
+                multiply(j, mine(band), blocks * lane, False)
+
         for p in range(per):
             c_copy(j, p, 0).start()
+        sums(sum_rest, jnp.maximum(last_sums(j - 1), j - 2), last_sums(j))
         return 0
 
     lax.fori_loop(0, chunks, step, 0)
-    lax.fori_loop(first_sums(chunks - 1), chunks, sum_first, 0)
-    lax.fori_loop(last_sums(chunks - 1), chunks, sum_rest, 0)
+
+    def take_lent(d):
+        lend_copy(d).wait_recv()
+
+        def one(g, _):
+            at = pl.ds(pl.multiple_of(g * lane, lane), lane)
+            value = lent[d, :, at]
+            high = value.astype(jnp.bfloat16)
+            hhi[d * rows:(d + 1) * rows, at] = high
+            hlo[d * rows:(d + 1) * rows, at] = (value - high.astype(jnp.float32)).astype(jnp.bfloat16)
+            return 0
+
+        lax.fori_loop(0, lent.shape[2] // lane, one, 0)
+
+    def extra(i, _):
+        j = chunks + i
+        take_part(i, 0).start()
+        sums(sum_first, first_sums(j - 1), first_sums(j))
+        settle(j - slots)
+        take_part(i, 0).wait()
+        split_b(0, part_rows, 0, part_rows)
+        multiply(j, theirs((bands - 1) * blocks * lane, blocks * part_rows), blocks * part_rows, True)
+        for k in range(1, bands):
+            take_b(i, (near + k) % bands, k % 2).start()
+            if k == 1:
+                sums(sum_rest, last_sums(j - 1), last_sums(j))
+            take_b(i, (near + k) % bands, k % 2).wait()
+            split_b(k % 2)
+            multiply(j, theirs((k - 1) * blocks * lane, blocks * lane), blocks * lane, False)
+        for p in range(per):
+            c_copy(j, p, 0).start()
+        return 0
+
+    if given:
+        @pl.when(helps)
+        def _():
+            for d in range(classes):
+                take_lent(d)
+            lax.fori_loop(0, given, extra, 0)
+
+    def last(k, _):
+        reduce(k, 0)
+
+        @pl.when(k > last_sums(total - 1))
+        def _():
+            sum_rest(k - 1, 0)
+
+        return 0
+
+    lax.fori_loop(first_sums(total - 1), total, last, 0)
+    sum_rest(total - 1, 0)
+
+    if given:
+        @pl.when(outer)
+        def _():
+            for i in range(given):
+                back_copy(i).wait_recv()
+                for p in range(per):
+                    at = pl.ds(i * per + p, rows, stride=ncol)
+                    rows_of[at, :] = rows_of[at, :] + back[i, p]
+            for g in range(late):
+                out_copy(g).start()
+
     for g in range(o_sem.shape[0]):
         out_copy(g).wait()
 
     def finish(j, _):
         own_mate(j).wait_send()
-        for p in range(per):
-            for level in range(levels):
-                c_copy(j, p, level).wait_send()
         for side in range(2):
-            @pl.when(has[side])
+            @pl.when(feeds(j, side))
             def _():
                 own_line(j, side).wait_send()
             for dist in range(1, spots):
-                @pl.when(there(side, dist))
+                @pl.when(gets(j, side, dist))
                 def _():
-                    @pl.when(has[side])
+                    @pl.when(feeds(j, side))
                     def _():
                         onward(j, side, dist).wait_send()
                     across(j, side, dist).wait_send()
         return 0
 
     lax.fori_loop(0, chunks, finish, 0)
+
+    def settled(j, _):
+        settle(j)
+        return 0
+
+    lax.fori_loop(total - slots, total, settled, 0)
     for d in range(1, classes):
         a_copy(d).wait_send()
+    if given:
+        @pl.when(outer)
+        def _():
+            for d in range(classes):
+                lend_copy(d).wait_send()
+
+        @pl.when(helps)
+        def _():
+            for i in range(given):
+                back_copy(i).wait_send()
 
 
 def streamed(classes, subs, first_factor_tiles, b_blocks):
@@ -684,8 +913,11 @@
     dma = pltpu.SemaphoreType.DMA
     f32, bf16 = jnp.float32, jnp.bfloat16
     spots, levels = subs // 2, classes.bit_length() - 1
+    given = chunks * GIVEN // 16 if spots > 3 and spots == 2 * bands and blocks % 2 == 0 else 0
+    deep = (2 * bands - 1) * blocks * lane // 2
+    some = max(given, 1)
     out, _, _ = pl.pallas_call(
-        functools.partial(stream, classes, subs),
+        functools.partial(stream, classes, subs, given),
         out_shape=(
             jax.ShapeDtypeStruct((rows, ncol, lane), f32),
             jax.ShapeDtypeStruct((classes - 1, lead, unit, lane), f32),
@@ -702,24 +934,32 @@
             pltpu.VMEM((2, blocks, lane, width), f32),
             pltpu.VMEM((blocks * lane, width), bf16),
             pltpu.VMEM((blocks * lane, width), bf16),
-            pltpu.VMEM((chunks, per, classes, rows, lane), f32),
-            pltpu.VMEM((chunks, per, classes - 1, rows, lane), f32),
+            pltpu.VMEM((min(SLOTS, chunks), per, classes, rows, lane), f32),
+            pltpu.VMEM((chunks + given, per, classes - 1, rows, lane), f32),
+            pltpu.VMEM((classes, rows, deep), f32),
+            pltpu.VMEM((classes * rows, deep), bf16),
+            pltpu.VMEM((classes * rows, deep), bf16),
+            pltpu.VMEM((some, per, rows, lane), f32),
             dma((classes,)),
             dma((classes,)),
+            dma((classes,)),
+            dma((classes,)),
+            dma((some,)),
+            dma((some,)),
             dma((2, chunks)),
             dma((2, chunks, spots)),
             dma((2, chunks, spots)),
             dma((chunks, spots)),
             dma((chunks, spots)),
             dma((chunks,)),
-            dma((chunks, per, levels)),
-            dma((chunks, per, levels)),
+            dma((chunks + given, per, levels)),
+            dma((chunks + given, per, levels)),
             dma((2,)),
             dma((2,)),
             dma((ncol // sub,)),
         ],
         compiler_params=pltpu.CompilerParams(
-            collective_id=0, has_side_effects=True, vmem_limit_bytes=60 * 1024 * 1024
+            collective_id=0, has_side_effects=True, vmem_limit_bytes=62 * 1024 * 1024
         ),
     )(left, right)
     out = out.reshape(rows, halves, wide // lane, cols, lane)

time: 325 us -> 303 us (0.932)
  Pallas kernels: 318 us -> 296 us
    pallas_call x1, Pallas kernels: 318 us -> 296 us  [streamed(): pl.pallas_call(functools.partial(stream, classes, subs, given), out_shape...]
where the time goes in v3:
time: 303 us; the launch traced here: 301 us
  Pallas kernels  296 us (98%)
  local copies, waits for them, and re-layouts  5.24 us (2%)
    pallas_call x1, Pallas kernels, streamed(): pl.pallas_call(functools.partial(stream, classes, subs, given), out_shape...  296 us

profile of v3, /device:TPU:0, one launch (start us, length us, event | category | flops | bytes accessed | tf_op | source)
XLA Modules:
  0.0 301.2 jit_solution(14427421249737511891)
XLA Ops:
  0.0 295.9 %shard_map.28 = (f32[256,32,128]{2,1,0:T(8,128)}, f32[3,512,8,128]{3,2,1,0:T(8,128)}, f32[16,8,256,256]{3,2,1,0:T(8,128)}) custom-call(f32[512,4,8,128]{3,2,1,0:T(8,128)} %bitcast.15, f32[256,32,128]{2,1,0:T(8,128)} %bitcast.16), custom_call_target="tpu_custom_call" | custom-call | tf_op jit(solution)/shard_map/pallas_call | solution.py:919
  295.9 5.2 %copy.7 = f32[8,32,2,4,512]{4,3,2,1,0:T(4,128)} copy(f32[8,32,2,4,512]{4,3,2,1,0:T(4,128)} %bitcast.17) | data formatting | bytes 8388608

commit v4 on v3

--- a/solution.py
+++ b/solution.py
@@ -11,6 +11,9 @@
 LAG = 3
 EARLY = 2
 AHEAD = 7
+OUTER = 3
+EARLY_RELAYS = ((3, 2), (5, 3), (7, 5))
+TURN = 1
 LEAD = 2
 MORE = 2
 GIVEN = 2
@@ -421,11 +424,24 @@
 
                 across(j, side, dist).start()
 
-    def relay(t):
+    def relay(t, _):
         for dist in range(1, spots):
-            @pl.when((t - dist + 1 >= 0) & (t - dist + 1 < chunks))
-            def _():
-                forward(t - dist + 1, dist)
+            at = jnp.where(inner, t - dist + 1, t)
+
+            @pl.when((at >= 0) & (at < chunks))
+            def _():
+                forward(at, dist)
+
+        @pl.when(inner & (t + LEAD < chunks))
+        def _():
+            own_out(t + LEAD)
+
+        return 0
+
+    def ready(t):
+        slow = jnp.maximum(t + 1, given + OUTER + (t + 1) // 2)
+        fast = AHEAD + 1 + (3 * t) // 4
+        return jnp.minimum(jnp.where(inner, jnp.maximum(fast, t + spots), slow), chunks + spots - 2)
 
     def feeds(j, side):
         return has[side] & ((j >= given) | jnp.logical_not(ends[side]))
@@ -547,29 +563,20 @@
     split_a(0)
     lend(0)
 
-    @pl.when(inner)
-    def _():
-        def early(j, _):
-            relay(j)
-
-            @pl.when(j + LEAD < chunks)
-            def _():
-                own_out(j + LEAD)
-
-            return 0
-
-        lax.fori_loop(0, min(AHEAD, chunks), early, 0)
-
-    for d in range(1, classes):
+    def accept(d):
         a_copy(d).wait_recv()
         take_a(d).start()
-        if d > 1:
-            take_a(d - 1).wait()
-            split_a(d - 1)
-            lend(d - 1)
-    take_a(classes - 1).wait()
-    split_a(classes - 1)
-    lend(classes - 1)
+        take_a(d).wait()
+        split_a(d)
+        lend(d)
+
+    at = [jnp.where(inner, x, y) for x, y in EARLY_RELAYS]
+    stops = [0] + [jnp.minimum(x, ready(-1)) for x in at]
+    for d in range(1, classes):
+        if d <= len(at):
+            lax.fori_loop(stops[d - 1], stops[d], relay, 0)
+        accept(d)
+    lax.fori_loop(stops[min(len(at), classes - 1)], ready(-1), relay, 0)
 
     def order(p):
         return [(p + i) % levels for i in range(levels)]
@@ -594,6 +601,14 @@
     def out_copy(g):
         at = pl.ds(pl.multiple_of(g * share, share), share)
         return pltpu.make_async_copy(flat.at[:, at, :], o_ref.at[:, at, :], o_sem.at[g])
+
+    turn = jnp.where(helps, chunks - TURN, chunks)
+
+    def chunk_of(t):
+        return jnp.where(helps & (t >= turn + given), t - given, t)
+
+    def lent_at(t):
+        return helps & (t >= turn) & (t < turn + given)
 
     late = -(-given * per // share)
 
@@ -612,27 +627,28 @@
                 c_copy(j, p, level + 1).start()
                 continue
 
-            @pl.when(j < chunks)
-            def _():
-                rows_of[pl.ds(j * per + p, rows, stride=ncol), :] = (
+            @pl.when(jnp.logical_not(lent_at(j)))
+            def _():
+                rows_of[pl.ds(chunk_of(j) * per + p, rows, stride=ncol), :] = (
                     cpart[held, p, 0] + rland[j, p, classes - 2]
                 )
 
             if given:
-                @pl.when(j >= chunks)
+                @pl.when(lent_at(j))
                 def _():
-                    back[j - chunks, p] = cpart[held, p, 0] + rland[j, p, classes - 2]
+                    back[j - turn, p] = cpart[held, p, 0] + rland[j, p, classes - 2]
         if level + 1 == levels:
-            group = (j + 1) // (share // per) - 1
-
-            @pl.when((j < chunks) & ((j + 1) % (share // per) == 0) & (inner | (group >= late)))
+            count, done = share // per, chunk_of(j) + 1
+            group = done // count - 1
+
+            @pl.when(jnp.logical_not(lent_at(j)) & (done % count == 0) & (inner | (group >= late)))
             def _():
                 out_copy(group).start()
 
             if given:
-                @pl.when(j >= chunks)
+                @pl.when(lent_at(j))
                 def _():
-                    back_copy(j - chunks).start()
+                    back_copy(j - turn).start()
 
     def gather(j, band):
         for owner in range(subs):
@@ -726,19 +742,9 @@
     def sums(body, begin, end):
         lax.fori_loop(begin, jnp.maximum(begin, end), body, 0)
 
-    def step(j, _):
-        @pl.when(inner)
-        def _():
-            relay(j + AHEAD)
-
-            @pl.when(j + AHEAD + LEAD < chunks)
-            def _():
-                own_out(j + AHEAD + LEAD)
-
-        @pl.when(outer)
-        def _():
-            forward(j, 1)
-
+    def usual(t):
+        j = chunk_of(t)
+        lax.fori_loop(ready(j - 1), ready(j), relay, 0)
         alone = outer & (j < given)
         whole = inner | (j >= given)
         gather(j, near)
@@ -747,16 +753,21 @@
         def _():
             take_b(j, near, 0).start()
 
+        @pl.when(inner)
+        def _():
+            gather(j, (near + 1) % bands)
+            take_b(j, (near + 1) % bands, 1).start()
+
         if given:
             @pl.when(alone)
             def _():
                 take_part(j, 0).start()
 
-        sums(sum_first, first_sums(j - 1), j - 1)
-
-        @pl.when(j >= slots)
-        def _():
-            settle(j - slots)
+        sums(sum_first, first_sums(t - 1), t - 1)
+
+        @pl.when(t >= slots)
+        def _():
+            settle(t - slots)
 
         @pl.when(whole)
         def _():
@@ -770,32 +781,28 @@
                 split_b(0, part_rows, (spot % 2) * part_rows)
                 clear_part((1 - spot % 2) * part_rows)
 
-        multiply(j, mine(near), blocks * lane, True)
-        sums(sum_first, jnp.maximum(j - 1, 0), first_sums(j))
-
-        @pl.when(outer)
-        def _():
-            for dist in range(2, spots):
-                forward(j, dist)
-
-        sums(sum_rest, last_sums(j - 1), j - 2)
+        multiply(t, mine(near), blocks * lane, True)
+        sums(sum_first, jnp.maximum(t - 1, 0), first_sums(t))
 
         @pl.when(whole)
         def _():
             for k in range(1, bands):
                 band = (near + k) % bands
-                gather(j, band)
-                take_b(j, band, k % 2).start()
+
+                @pl.when(outer | (k > 1))
+                def _():
+                    gather(j, band)
+                    take_b(j, band, k % 2).start()
+
+                if k == 1:
+                    sums(sum_rest, last_sums(t - 1), t - 2)
                 take_b(j, band, k % 2).wait()
                 split_b(k % 2)
-                multiply(j, mine(band), blocks * lane, False)
-
-        for p in range(per):
-            c_copy(j, p, 0).start()
-        sums(sum_rest, jnp.maximum(last_sums(j - 1), j - 2), last_sums(j))
-        return 0
-
-    lax.fori_loop(0, chunks, step, 0)
+                multiply(t, mine(band), blocks * lane, False)
+
+        @pl.when(alone)
+        def _():
+            sums(sum_rest, last_sums(t - 1), t - 2)
 
     def take_lent(d):
         lend_copy(d).wait_recv()
@@ -810,31 +817,51 @@
 
         lax.fori_loop(0, lent.shape[2] // lane, one, 0)
 
-    def extra(i, _):
-        j = chunks + i
+    def extra(t):
+        i = t - turn
         take_part(i, 0).start()
-        sums(sum_first, first_sums(j - 1), first_sums(j))
-        settle(j - slots)
+        for k in range(1, bands):
+            if k == 1:
+                take_b(i, (near + k) % bands, k % 2).start()
+        sums(sum_first, first_sums(t - 1), first_sums(t))
+
+        @pl.when(t >= slots)
+        def _():
+            settle(t - slots)
+
+        @pl.when(i == 0)
+        def _():
+            for d in range(classes):
+                take_lent(d)
+
         take_part(i, 0).wait()
         split_b(0, part_rows, 0, part_rows)
-        multiply(j, theirs((bands - 1) * blocks * lane, blocks * part_rows), blocks * part_rows, True)
+        multiply(t, theirs((bands - 1) * blocks * lane, blocks * part_rows), blocks * part_rows, True)
         for k in range(1, bands):
-            take_b(i, (near + k) % bands, k % 2).start()
+            if k > 1:
+                take_b(i, (near + k) % bands, k % 2).start()
             if k == 1:
-                sums(sum_rest, last_sums(j - 1), last_sums(j))
+                sums(sum_rest, last_sums(t - 1), last_sums(t))
             take_b(i, (near + k) % bands, k % 2).wait()
             split_b(k % 2)
-            multiply(j, theirs((k - 1) * blocks * lane, blocks * lane), blocks * lane, False)
+            multiply(t, theirs((k - 1) * blocks * lane, blocks * lane), blocks * lane, False)
+
+    def step(t, _):
+        if given:
+            @pl.when(lent_at(t))
+            def _():
+                extra(t)
+
+        @pl.when(jnp.logical_not(lent_at(t)))
+        def _():
+            usual(t)
+
         for p in range(per):
-            c_copy(j, p, 0).start()
-        return 0
-
-    if given:
-        @pl.when(helps)
-        def _():
-            for d in range(classes):
-                take_lent(d)
-            lax.fori_loop(0, given, extra, 0)
+            c_copy(t, p, 0).start()
+        sums(sum_rest, jnp.maximum(last_sums(t - 1), t - 2), last_sums(t))
+        return 0
+
+    lax.fori_loop(0, total, step, 0)
 
     def last(k, _):
         reduce(k, 0)

time: 303 us -> 287 us (0.947)
  Pallas kernels: 296 us -> 280 us
    pallas_call x1, Pallas kernels: 296 us -> 280 us  [streamed(): pl.pallas_call(functools.partial(stream, classes, subs, given), out_shape...]
where the time goes in v4:
time: 287 us; the launch traced here: 285 us
  Pallas kernels  280 us (98%)
  local copies, waits for them, and re-layouts  5.24 us (2%)
    pallas_call x1, Pallas kernels, streamed(): pl.pallas_call(functools.partial(stream, classes, subs, given), out_shape...  280 us

profile of v4, /device:TPU:0, one launch (start us, length us, event | category | flops | bytes accessed | tf_op | source)
XLA Modules:
  0.0 285.2 jit_solution(15893853147917880275)
XLA Ops:
  0.0 279.9 %shard_map.28 = (f32[256,32,128]{2,1,0:T(8,128)}, f32[3,512,8,128]{3,2,1,0:T(8,128)}, f32[16,8,256,256]{3,2,1,0:T(8,128)}) custom-call(f32[512,4,8,128]{3,2,1,0:T(8,128)} %bitcast.15, f32[256,32,128]{2,1,0:T(8,128)} %bitcast.16), custom_call_target="tpu_custom_call" | custom-call | tf_op jit(solution)/shard_map/pallas_call | solution.py:946
  279.9 5.2 %copy.7 = f32[8,32,2,4,512]{4,3,2,1,0:T(4,128)} copy(f32[8,32,2,4,512]{4,3,2,1,0:T(4,128)} %bitcast.17) | data formatting | bytes 8388608

commit v5 on v4

--- a/solution.py
+++ b/solution.py
@@ -11,14 +11,15 @@
 LAG = 3
 EARLY = 2
 AHEAD = 7
-OUTER = 3
+OUTER = 2
 EARLY_RELAYS = ((3, 2), (5, 3), (7, 5))
 TURN = 1
+BLOCK = 2
 LEAD = 2
 MORE = 2
 GIVEN = 2
 SLOTS = 8
-CALM = 14
+CALM = 15
 LANE = 128
 SUBLANE = 8
 
@@ -363,8 +364,14 @@
         @pl.when(has[side])
         def _():
             pl.semaphore_signal(barrier, inc=1, device_id=beside[side], device_id_type=MESH)
-    b_in = pltpu.make_async_copy(b_ref, flat, b_load.at[0])
-    b_in.start()
+    share = ncol // o_sem.shape[0]
+
+    def b_in(g):
+        at = pl.ds(g * share, share)
+        return pltpu.make_async_copy(b_ref.at[:, at, :], flat.at[:, at, :], o_sem.at[g])
+
+    for g in range(o_sem.shape[0]):
+        b_in(g).start()
     lower, higher = (spot + spots - 1) // spots, (2 * spots - 2 - spot) // spots
     pl.semaphore_wait(barrier, classes + lower + higher)
 
@@ -425,10 +432,10 @@
                 across(j, side, dist).start()
 
     def relay(t, _):
-        for dist in range(1, spots):
-            at = jnp.where(inner, t - dist + 1, t)
-
-            @pl.when((at >= 0) & (at < chunks))
+        for dist in reversed(range(1, spots)):
+            at = t - dist + 1 if dist > 1 else t
+
+            @pl.when((at >= 0) & (at < chunks) & (inner | (dist == 1)))
             def _():
                 forward(at, dist)
 
@@ -437,6 +444,18 @@
             own_out(t + LEAD)
 
         return 0
+
+    def relay_far(t, _):
+        @pl.when(outer & (t < chunks))
+        def _():
+            for dist in range(2, spots):
+                forward(t, dist)
+
+        return 0
+
+    def relay_all(t, _):
+        relay(t, 0)
+        return relay_far(t, 0)
 
     def ready(t):
         slow = jnp.maximum(t + 1, given + OUTER + (t + 1) // 2)
@@ -461,7 +480,6 @@
             def _():
                 own_line(j + shift, side).start()
 
-    b_in.wait()
     rows_of = flat.reshape(rows * ncol, lane)
 
     def lay(j):
@@ -470,15 +488,25 @@
             bown[j, :, :, p * lane:(p + 1) * lane] = value.reshape(blocks, piece, lane)
 
     first = min(LEAD + shift, chunks)
+    opened = 0
     for j in range(first):
+        if j * per // share == opened:
+            b_in(opened).wait()
+            opened += 1
         lay(j)
-    for side in range(2):
-        for j in range(given, min(given + MORE, chunks)):
-            @pl.when(ends[side])
-            def _():
-                own_line(j, side).start()
-    for j in range(min(LEAD, chunks)):
-        own_out(j)
+        for side in range(2):
+            if j < LEAD:
+                @pl.when(has[side] & jnp.logical_not(ends[side]))
+                def _():
+                    own_line(j, side).start()
+
+            if j >= given:
+                @pl.when(ends[side])
+                def _():
+                    own_line(j, side).start()
+
+    for g in range(opened, o_sem.shape[0]):
+        b_in(g).wait()
 
     def lay_more(j, _):
         lay(j)
@@ -574,9 +602,9 @@
     stops = [0] + [jnp.minimum(x, ready(-1)) for x in at]
     for d in range(1, classes):
         if d <= len(at):
-            lax.fori_loop(stops[d - 1], stops[d], relay, 0)
+            lax.fori_loop(stops[d - 1], stops[d], relay_all, 0)
         accept(d)
-    lax.fori_loop(stops[min(len(at), classes - 1)], ready(-1), relay, 0)
+    lax.fori_loop(stops[min(len(at), classes - 1)], ready(-1), relay_all, 0)
 
     def order(p):
         return [(p + i) % levels for i in range(levels)]
@@ -595,8 +623,6 @@
             rland.at[j, p, pl.ds(classes - 2 * count, count)],
             c_send.at[j, p, level], c_recv.at[j, p, level], (peer, s),
         )
-
-    share = ncol // o_sem.shape[0]
 
     def out_copy(g):
         at = pl.ds(pl.multiple_of(g * share, share), share)
@@ -704,17 +730,18 @@
         dot = functools.partial(jnp.dot, preferred_element_type=jnp.float32)
         held = j % slots
 
-        def part(d, _):
-            at = pl.ds(pl.multiple_of(d * rows, rows), rows)
+        def part(i, _):
+            at = pl.ds(pl.multiple_of(i * BLOCK * rows, rows), BLOCK * rows)
             high, low = left(at)
             total = dot(high, bhi[0:deep]) + dot(high, blo[0:deep]) + dot(low, bhi[0:deep])
             for p in range(per):
-                value = total[:, p * lane:(p + 1) * lane]
-                to = place(p, d)
-                cpart[held, p, to] = value if first else cpart[held, p, to] + value
+                for k in range(BLOCK):
+                    value = total[k * rows:(k + 1) * rows, p * lane:(p + 1) * lane]
+                    to = place(p, i * BLOCK + k)
+                    cpart[held, p, to] = value if first else cpart[held, p, to] + value
             return 0
 
-        lax.fori_loop(0, classes, part, 0)
+        lax.fori_loop(0, classes // BLOCK, part, 0)
 
     def mine(band):
         return lambda at: (ahi[band, at, :], alo[band, at, :])
@@ -783,6 +810,7 @@
 
         multiply(t, mine(near), blocks * lane, True)
         sums(sum_first, jnp.maximum(t - 1, 0), first_sums(t))
+        lax.fori_loop(ready(j - 1), ready(j), relay_far, 0)
 
         @pl.when(whole)
         def _():

time: 287 us -> 281 us (0.979)
  Pallas kernels: 280 us -> 275 us
    pallas_call x1, Pallas kernels: 280 us -> 275 us  [streamed(): pl.pallas_call(functools.partial(stream, classes, subs, given), out_shape...]
where the time goes in v5:
time: 281 us; the launch traced here: 280 us
  Pallas kernels  275 us (98%)
  local copies, waits for them, and re-layouts  5.24 us (2%)
    pallas_call x1, Pallas kernels, streamed(): pl.pallas_call(functools.partial(stream, classes, subs, given), out_shape...  275 us

profile of v5, /device:TPU:0, one launch (start us, length us, event | category | flops | bytes accessed | tf_op | source)
XLA Modules:
  0.0 279.8 jit_solution(7630370686793586669)
XLA Ops:
  0.0 274.5 %shard_map.28 = (f32[256,32,128]{2,1,0:T(8,128)}, f32[3,512,8,128]{3,2,1,0:T(8,128)}, f32[16,8,256,256]{3,2,1,0:T(8,128)}) custom-call(f32[512,4,8,128]{3,2,1,0:T(8,128)} %bitcast.15, f32[256,32,128]{2,1,0:T(8,128)} %bitcast.16), custom_call_target="tpu_custom_call" | custom-call | tf_op jit(solution)/shard_map/pallas_call | solution.py:974
  274.5 5.2 %copy.7 = f32[8,32,2,4,512]{4,3,2,1,0:T(4,128)} copy(f32[8,32,2,4,512]{4,3,2,1,0:T(4,128)} %bitcast.17) | data formatting | bytes 8388608
